TPU v7x, 512 devices: a 4x2x32 block of a 4x8x32 slice. The times are simulated.
512 devices in a mesh: groups: 2 (over y), dp: 4 (over x), tensor: 64 (over z, core).
Axes of the slice: x: 4, y: 2, z: 32, core: 2. Of those that a mesh axis runs over, the one named last changes fastest.
The devices are a block of a 4x8x32 slice.
Arguments:
- tokens: bfloat16 [1024, 8192], P(('groups', 'dp'), 'tensor'), parts along dimension 0, may hold values from -6 to 6
- gate_up_weight: bfloat16 [8192, 32768], P('dp', 'tensor'), may hold values from -0.0625 to 0.0625
- down_weight: bfloat16 [16384, 8192], P('tensor', 'dp'), may hold values from -0.046875 to 0.046875
Outputs:
- mixed_out: bfloat16 [1024, 8192], P(('groups', 'dp'), 'tensor'), parts along dimension 0
There are 2 independent parts, one for each index of `groups`. A program takes and returns all parts, laid end to end along the dimension named above; an argument that names none is the same for every part. Nothing has to cross between parts.
All inputs are finite; a program needn't handle non-finite values.
Results may differ from a plain program's by a relative error of at most 0.0049.
Values may be sent and summed in bfloat16 or wider, within the bound.
No kernel may reach another device: no remote copies, remote signals or barrier semaphores. Data moves between devices by JAX's collectives and lax.ppermute only.
A program may use at most 64 MiB of HBM per device.

v0:
```python
import jax
import jax.numpy as jnp
from jax import lax
from jax.sharding import Mesh
from jax.sharding import PartitionSpec as P

TENSOR = ("tensor_0", "tensor_1")


def split_up(array, dim, devices):
    lengths = array.shape
    pieces = array.reshape(*lengths[:dim], devices, lengths[dim] // devices, *lengths[dim + 1 :])
    return jnp.moveaxis(pieces, dim, 0)


def summed_on_arrival(array, axis, dim):
    pieces = split_up(array, dim, lax.axis_size(axis))
    arrived = lax.all_to_all(pieces, axis, split_axis=0, concat_axis=0, tiled=True)
    return arrived.sum(axis=0)


def reduced_to_own(pieces, axes, turns):
    lengths = [lax.axis_size(a) for a in axes]
    pieces = pieces.reshape(*lengths, *pieces.shape[1:])
    pieces = pieces.transpose(*turns, *range(len(axes), pieces.ndim))
    pieces = pieces.reshape(-1, *pieces.shape[len(axes) :])
    for k in turns:
        pieces = lax.psum_scatter(pieces, axes[k], scatter_dimension=0, tiled=True)
    return pieces[0]


def summed_rows(array, axes, turns, dim):
    devices = lax.axis_size(axes)
    return reduced_to_own(split_up(array, dim, devices), axes, turns)


def per_device(tokens, gate_up_weight, down_weight):
    whole = lax.all_gather(tokens, TENSOR, axis=1, tiled=True)
    blocks = lax.all_to_all(whole, "dp", split_axis=1, concat_axis=0, tiled=True)
    partial_value = jnp.dot(blocks, gate_up_weight, preferred_element_type=jnp.float32)
    combined = summed_on_arrival(partial_value, "dp", 0)
    gate_part = combined[:, 0::2]
    up_part = combined[:, 1::2]
    hidden = (jax.nn.silu(gate_part) * up_part).astype(jnp.bfloat16)
    terms = jnp.dot(
        hidden,
        lax.all_gather(down_weight, "dp", axis=1, tiled=True),
        preferred_element_type=jnp.float32,
    )
    result = summed_rows(terms, TENSOR, (1, 0), 1).astype(jnp.bfloat16)
    return result


def solution(mesh):
    split = Mesh(
        mesh.devices.reshape(mesh.shape["groups"], mesh.shape["dp"], 32, 2),
        ("groups", "dp", "tensor_0", "tensor_1"),
    )
    placed = (P(("groups", "dp"), TENSOR), P("dp", TENSOR), P(TENSOR, "dp"))
    return jax.shard_map(
        per_device,
        mesh=split,
        in_specs=placed,
        out_specs=P(("groups", "dp"), TENSOR),
        check_vma=False,
    )
```

profile of v0, /device:TPU:34, one launch (start us, length us, event | category | flops | bytes accessed | tf_op | source)
XLA Modules:
  0.0 427.3 jit_solution(7535571929986580808)
XLA Ops:
  6.5 0.0 copy-start
  6.6 0.0 all-gather.3.cloned.1.call-start
  6.6 1.6 copy.5
  8.2 0.1 all-gather.3.cloned.1.call-update
  8.2 0.1 all-gather.5.cloned.1.call-start
  8.3 0.7 all-gather.5.cloned.1.call-update
  9.1 0.1 reduce-scatter.3.cloned.1.call-start
  9.1 160.0 %all-gather.3.cloned.1.call-done = bf16[128,8192]{0,1:T(8,128)(2,1)} async-done(((bf16[128,128]{0,1:T(8,128)(2,1)}), bf16[128,8192]{0,1:T(8,128)(2,1)}) %all-gather.3.cloned.1.call-update) | async-done | bytes 2097168 | tf_op jit(solution)/shard_map/all_gather | solution.py:38
  169.1 4.0 copy.6
  173.1 41.2 %all_to_all.21 = bf16[128,4,2048]{2,0,1:T(8,128)(2,1)S(1)} all-to-all(bf16[128,4,2048]{2,0,1:T(8,128)(2,1)} %copy.6), channel_id=1, replica_groups=mesh['groups'=2,'dp'=4,'tensor_0'=32,'tensor_1'=2] {'dp'}, dimensions={1} | all-to-all | bytes 4194304 | tf_op jit(solution)/shard_map/all_to_all | solution.py:39
  214.3 0.0 copy-done
  214.3 1.2 fusion
  215.5 29.6 %all_to_all.22 = f32[4,128,512]{2,1,0:T(8,128)S(1)} all-to-all(f32[4,128,512]{2,1,0:T(8,128)S(1)} %fusion), channel_id=1, replica_groups=mesh['groups'=2,'dp'=4,'tensor_0'=32,'tensor_1'=2] {'dp'}, dimensions={0} | all-to-all | bytes 2097152 | tf_op jit(solution)/shard_map/all_to_all | solution.py:18
  245.1 0.1 reduce_sum.9
  245.2 4.5 %slice.7 = f32[128,256]{1,0:T(8,128)S(1)} slice(f32[128,512]{1,0:T(8,128)S(1)} %reduce_sum.9), slice={[0:128:1], [1:512:2]} | slice | bytes 262144 | tf_op jit(solution)/shard_map/slice | solution.py:43
  249.7 4.5 %slice.6 = f32[128,256]{1,0:T(8,128)S(1)} slice(f32[128,512]{1,0:T(8,128)S(1)} %reduce_sum.9), slice={[0:128:1], [0:512:2]} | slice | bytes 262144 | tf_op jit(solution)/shard_map/slice | solution.py:42
  254.2 0.0 all-gather.5.cloned.1.call-done
  254.2 2.9 convolution_bitcast_fusion
  257.2 0.7 copy.8
  257.9 4.4 %copy.7 = f32[32,2,128,128]{3,2,0,1:T(8,128)} copy(f32[32,2,128,128]{3,1,0,2:T(2,128)S(1)} %bitcast.21) | data formatting | bytes 8388608 | tf_op jit(solution)/shard_map/reshape | solution.py:24
  262.3 0.1 reduce-scatter.3.cloned.1.call-update
  262.3 0.1 reduce-scatter.5.cloned.1.call-start
  262.4 15.9 %reduce-scatter.3.cloned.1.call-done = f32[32,128,128]{2,1,0:T(8,128)} async-done(((f32[64,128,128]{2,1,0:T(8,128)}), f32[32,128,128]{2,1,0:T(8,128)}) %reduce-scatter.3.cloned.1.call-update) | async-done | bytes 2097168 | tf_op jit(solution)/shard_map/reduce_scatter | solution.py:28
  278.3 0.1 reduce-scatter.5.cloned.1.call-update
  278.4 141.0 %reduce-scatter.5.cloned.1.call-done = f32[1,128,128]{2,1,0:T(8,128)} async-done(((f32[32,128,128]{2,1,0:T(8,128)}), f32[1,128,128]{2,1,0:T(8,128)}) %reduce-scatter.5.cloned.1.call-update) | async-done | bytes 65552 | tf_op jit(solution)/shard_map/reduce_scatter | solution.py:28
  419.3 1.5 convert_bitcast_fusion
Async XLA Ops:
  6.5 207.8 %copy-start = (bf16[2048,512]{1,0:T(8,128)(2,1)S(1)}, bf16[2048,512]{1,0:T(8,128)(2,1)}, u32[]{:S(2)}) copy-start(bf16[2048,512]{1,0:T(8,128)(2,1)} %param.4) | copy-start | bytes 6291460
  6.6 162.5 %all-gather.3.cloned.1.call-start = ((), (), s32[]{:S(2)}) async-start(), calls=%async_computation.4 | async-start | bytes 2129920 | tf_op jit(solution)/shard_map/all_gather | solution.py:38
  8.2 246.0 %all-gather.5.cloned.1.call-start = ((), (), s32[]{:S(2)}) async-start(), calls=%async_computation.5 | async-start | bytes 5242880 | tf_op jit(solution)/shard_map/all_gather | solution.py:47
  9.1 269.2 %reduce-scatter.3.cloned.1.call-start = ((), (), s32[]{:S(2)}) async-start(), calls=%async_computation.6 | async-start | bytes 6291456 | tf_op jit(solution)/shard_map/reduce_scatter | solution.py:28
  262.3 157.0 %reduce-scatter.5.cloned.1.call-start = ((), (), s32[]{:S(2)}) async-start(), calls=%async_computation.7 | async-start | bytes 2162688 | tf_op jit(solution)/shard_map/reduce_scatter | solution.py:28
Sparse Core Ops, SparseCore 0:
  9.5 159.5 all-gather.2
  171.2 76.5 all-gather.4
  262.5 15.7 reduce-scatter.2
  281.0 138.3 reduce-scatter.4
where the time goes:
time: 428 us; the launch traced here: 427 us
  waiting for transfers between devices  318 us (74%)
  blocking collectives  70.8 us (17%)
  local copies, waits for them, and re-layouts  19.7 us (5%)
  between operations  13.2 us (3%)
    all_gather x1, waiting for transfers between devices, per_device(): whole = lax.all_gather(tokens, TENSOR, axis=1, tiled=True)  160 us
    reduce_scatter x2, waiting for transfers between devices, reduced_to_own(): pieces = lax.psum_scatter(pieces, axes[k], scatter_dimension=0, tiled=True)  157 us
    all_to_all x1, blocking collectives, per_device(): lax.all_to_all(whole, 'dp', split_axis=1, concat_axis=0, tiled=True)  41.2 us
    all_to_all x1, blocking collectives, summed_on_arrival(): lax.all_to_all(pieces, axis, split_axis=0, concat_axis=0, tiled=True)  29.6 us
  transfers between devices with their start and end apart: 4, of which 3 were waited for; matrix products, arithmetic and copies ran while one was open for 3% of the time, Pallas kernels for 0%

commit v1 on v0

--- a/solution.py
+++ b/solution.py
@@ -5,6 +5,18 @@
 from jax.sharding import PartitionSpec as P
 
 TENSOR = ("tensor_0", "tensor_1")
+
+
+def knots_create(bus_axis, raw):
+    return jnp.concatenate(
+        lax.all_to_all(
+            jnp.stack([raw for _ in range(lax.axis_size(bus_axis))], axis=0),
+            axis_name=bus_axis,
+            split_axis=0,
+            concat_axis=0,
+        ),
+        1,
+    )
 
 
 def split_up(array, dim, devices):
@@ -35,7 +47,7 @@
 
 
 def per_device(tokens, gate_up_weight, down_weight):
-    whole = lax.all_gather(tokens, TENSOR, axis=1, tiled=True)
+    whole = knots_create(TENSOR, tokens)
     blocks = lax.all_to_all(whole, "dp", split_axis=1, concat_axis=0, tiled=True)
     partial_value = jnp.dot(blocks, gate_up_weight, preferred_element_type=jnp.float32)
     combined = summed_on_arrival(partial_value, "dp", 0)

time: 428 us -> 487 us (1.14)
  starting transfers between devices: 0.19 us -> 47.6 us
  waiting for transfers between devices: 318 us -> 357 us
  blocking collectives: 70.8 us -> 41.9 us
    all_to_all x0 -> x1, waiting for transfers between devices: none -> 198 us  [knots_create(): lax.all_to_all(jnp.stack([raw for _ in range(lax.axis_size(bus_axis))], a...]
    all_gather x1 -> x0, waiting for transfers between devices: 160 us -> none  [per_device(): whole = lax.all_gather(tokens, TENSOR, axis=1, tiled=True)]
    all_to_all x0 -> x1, starting transfers between devices: none -> 47.4 us  [knots_create(): lax.all_to_all(jnp.stack([raw for _ in range(lax.axis_size(bus_axis))], a...]
    all_to_all x1, blocking collectives: 29.6 us -> 14.4 us  [summed_on_arrival(): lax.all_to_all(pieces, axis, split_axis=0, concat_axis=0, tiled=True)]
    all_to_all x1, blocking collectives: 41.2 us -> 27.5 us  [per_device(): lax.all_to_all(whole, 'dp', split_axis=1, concat_axis=0, tiled=True)]
where the time goes in v1:
time: 487 us
  waiting for transfers between devices  357 us (73%)
  starting transfers between devices  47.6 us (10%)
  blocking collectives  41.9 us (9%)
  local copies, waits for them, and re-layouts  21 us (4%)
  between operations  13.2 us (3%)
    all_to_all x1, waiting for transfers between devices, knots_create(): lax.all_to_all(jnp.stack([raw for _ in range(lax.axis_size(bus_axis))], a...  198 us
    reduce_scatter x2, waiting for transfers between devices, reduced_to_own(): pieces = lax.psum_scatter(pieces, axes[k], scatter_dimension=0, tiled=True)  158 us
    all_to_all x1, starting transfers between devices, knots_create(): lax.all_to_all(jnp.stack([raw for _ in range(lax.axis_size(bus_axis))], a...  47.4 us
    all_to_all x1, blocking collectives, per_device(): lax.all_to_all(whole, 'dp', split_axis=1, concat_axis=0, tiled=True)  27.5 us
    all_to_all x1, blocking collectives, summed_on_arrival(): lax.all_to_all(pieces, axis, split_axis=0, concat_axis=0, tiled=True)  14.4 us
  transfers between devices with their start and end apart: 4, of which 3 were waited for; matrix products, arithmetic and copies ran while one was open for 3% of the time, Pallas kernels for 0%

profile of v1, /device:TPU:34, one launch (start us, length us, event | category | flops | bytes accessed | tf_op | source)
XLA Modules:
  0.0 486.5 jit_solution(14032892724918325018)
XLA Ops:
  6.5 0.0 copy-start
  6.6 1.0 copy.5
  7.6 1.9 stack.2
  9.4 47.4 %all-to-all-start = ((bf16[64,128,128]{1,2,0:T(8,128)(2,1)}), bf16[64,128,128]{1,2,0:T(8,128)(2,1)}, u32[]{:S(2)}, u32[]{:S(2)}) async-start(bf16[64,128,128]{1,2,0:T(8,128)(2,1)} %stack.2), calls=%async_computation | async-start | bytes 4194304 | tf_op jit(solution)/shard_map/all_to_all | solution.py:12
  56.8 0.1 all-gather.2.cloned.1.call-start
  56.9 0.7 all-gather.2.cloned.1.call-update
  57.6 0.1 reduce-scatter.3.cloned.1.call-start
  57.7 198.2 %all-to-all-done = bf16[64,128,128]{1,2,0:T(8,128)(2,1)} async-done(((bf16[64,128,128]{1,2,0:T(8,128)(2,1)}), bf16[64,128,128]{1,2,0:T(8,128)(2,1)}, u32[]{:S(2)}, u32[]{:S(2)}) %all-to-all-start) | async-done | bytes 2097184 | tf_op jit(solution)/shard_map/all_to_all | solution.py:12
  255.9 4.0 copy.6
  259.9 27.5 %all_to_all.26 = bf16[128,4,2048]{2,0,1:T(8,128)(2,1)S(1)} all-to-all(bf16[128,4,2048]{2,0,1:T(8,128)(2,1)} %copy.6), channel_id=1, replica_groups=mesh['groups'=2,'dp'=4,'tensor_0'=32,'tensor_1'=2] {'dp'}, dimensions={1} | all-to-all | bytes 4194304 | tf_op jit(solution)/shard_map/all_to_all | solution.py:51
  287.5 0.0 copy-done
  287.5 1.2 fusion
  288.7 14.4 %all_to_all.27 = f32[4,128,512]{2,1,0:T(8,128)S(1)} all-to-all(f32[4,128,512]{2,1,0:T(8,128)S(1)} %fusion), channel_id=1, replica_groups=mesh['groups'=2,'dp'=4,'tensor_0'=32,'tensor_1'=2] {'dp'}, dimensions={0} | all-to-all | bytes 2097152 | tf_op jit(solution)/shard_map/all_to_all | solution.py:30
  303.1 0.1 reduce_sum.9
  303.2 4.5 slice.7
  307.7 4.5 slice.6
  312.2 0.0 all-gather.2.cloned.1.call-done
  312.2 2.9 convolution_bitcast_fusion
  315.1 0.7 copy.8
  315.9 4.4 copy.7
  320.3 0.1 reduce-scatter.3.cloned.1.call-update
  320.3 0.1 reduce-scatter.5.cloned.1.call-start
  320.4 17.1 %reduce-scatter.3.cloned.1.call-done = f32[32,128,128]{2,1,0:T(8,128)} async-done(((f32[64,128,128]{2,1,0:T(8,128)}), f32[32,128,128]{2,1,0:T(8,128)}) %reduce-scatter.3.cloned.1.call-update) | async-done | bytes 2097168 | tf_op jit(solution)/shard_map/reduce_scatter | solution.py:40
  337.5 0.1 reduce-scatter.5.cloned.1.call-update
  337.6 140.9 %reduce-scatter.5.cloned.1.call-done = f32[1,128,128]{2,1,0:T(8,128)} async-done(((f32[32,128,128]{2,1,0:T(8,128)}), f32[1,128,128]{2,1,0:T(8,128)}) %reduce-scatter.5.cloned.1.call-update) | async-done | bytes 65552 | tf_op jit(solution)/shard_map/reduce_scatter | solution.py:40
  478.5 1.5 convert_bitcast_fusion
Async XLA Ops:
  6.5 280.9 %copy-start = (bf16[2048,512]{1,0:T(8,128)(2,1)S(1)}, bf16[2048,512]{1,0:T(8,128)(2,1)}, u32[]{:S(2)}) copy-start(bf16[2048,512]{1,0:T(8,128)(2,1)} %param.4) | copy-start | bytes 6291460
  9.4 246.5 %all-to-all-start = ((bf16[64,128,128]{1,2,0:T(8,128)(2,1)}), bf16[64,128,128]{1,2,0:T(8,128)(2,1)}, u32[]{:S(2)}, u32[]{:S(2)}) async-start(bf16[64,128,128]{1,2,0:T(8,128)(2,1)} %stack.2), calls=%async_computation | async-start | bytes 4194304 | tf_op jit(solution)/shard_map/all_to_all | solution.py:12
  56.8 255.4 %all-gather.2.cloned.1.call-start = ((), (), s32[]{:S(2)}) async-start(), calls=%async_computation.5 | async-start | bytes 5242880 | tf_op jit(solution)/shard_map/all_gather | solution.py:59
  57.6 279.9 %reduce-scatter.3.cloned.1.call-start = ((), (), s32[]{:S(2)}) async-start(), calls=%async_computation.6 | async-start | bytes 6291456 | tf_op jit(solution)/shard_map/reduce_scatter | solution.py:40
  320.3 158.2 %reduce-scatter.5.cloned.1.call-start = ((), (), s32[]{:S(2)}) async-start(), calls=%async_computation.7 | async-start | bytes 2162688 | tf_op jit(solution)/shard_map/reduce_scatter | solution.py:40
Sparse Core Ops, SparseCore 0:
  59.7 64.2 all-gather.1
  320.4 17.0 reduce-scatter.2
  340.4 138.1 reduce-scatter.4
